TPU v7x, 32 devices: a 4x4x1 block of a 4x4x8 slice. The times are simulated.
32 devices in a mesh: batch: 1 (over z), row: 4 (over y), col: 8 (over x, core).
Axes of the slice: x: 4, y: 4, z: 1, core: 2. Of those that a mesh axis runs over, the one named last changes fastest.
The devices are a block of a 4x4x8 slice.
Arguments:
- spd_blocks: float32 [32, 256, 8192], P(('batch', 'row'), None, 'col')
Outputs:
- output: float32 [32, 256, 8192], P(('batch', 'row'), None, 'col')
All inputs are finite; a program needn't handle non-finite values.
Results may differ from a plain program's by a relative error of at most 0.001.
Values are sent between devices in bfloat16 or wider.
A program may use at most 768 MiB of HBM per device.

v0:
```python
import functools
import jax
import jax.numpy as jnp
from jax import lax
from jax.sharding import PartitionSpec as P, NamedSharding


def transposed_panel(row_panel, row_id, col_id, row_devs, col_devs, row_skip, col_skip):
    row_blocks = row_panel.shape[0]
    blk_size = row_panel.shape[1]
    if row_devs >= col_devs:
        grid_ratio = row_devs // col_devs
        blk_shift = (row_skip * row_devs - col_skip * col_devs) // col_devs
        pick_mask = (jnp.arange(grid_ratio) == row_id // col_devs) & (row_id % col_devs == col_id)
        spread = (row_panel[:, None] * pick_mask.astype(jnp.bfloat16)[None, :, None, None]).reshape(row_blocks * grid_ratio, blk_size, blk_size)
        if blk_shift >= 0:
            spread = jnp.pad(spread, ((blk_shift, 0), (0, 0), (0, 0)))
        else:
            spread = spread[-blk_shift:]
    else:
        grid_ratio = col_devs // row_devs
        blk_shift = (col_skip * col_devs - row_skip * row_devs) // row_devs
        if blk_shift >= 0:
            shifted = row_panel[blk_shift:]
        else:
            shifted = jnp.pad(row_panel, ((-blk_shift, 0), (0, 0), (0, 0)))
        grouped = shifted.reshape(shifted.shape[0] // grid_ratio, grid_ratio, blk_size, blk_size)
        chosen = lax.dynamic_index_in_dim(grouped, col_id // row_devs, axis=1, keepdims=False)
        spread = jnp.where(row_id == col_id % row_devs, chosen, jnp.zeros_like(chosen))
    return lax.psum(spread, "row")


def solution(mesh):
    row_devs = mesh.shape["row"]
    col_devs = mesh.shape["col"]

    def factor_local(a_loc):
        row_blocks, blk_size, local_cols = a_loc.shape
        col_blocks = local_cols // blk_size
        blk_count = row_blocks * row_devs
        row_id = lax.axis_index("row")
        col_id = lax.axis_index("col")
        eye_blk = jnp.eye(blk_size, dtype=jnp.float32)

        def panel_step(step_idx, window):
            win_rows, win_cols = window.shape
            win_rblk = win_rows // blk_size
            row_skip = row_blocks - win_rblk
            col_skip = col_blocks - win_cols // blk_size
            own_col = col_id == step_idx % col_devs
            is_owner = own_col & (row_id == step_idx % row_devs)
            col_off = (step_idx // col_devs - col_skip) * blk_size
            col_blk = lax.dynamic_slice_in_dim(window, col_off, blk_size, axis=1)
            diag_blk = lax.dynamic_slice_in_dim(col_blk, (step_idx // row_devs - row_skip) * blk_size, blk_size, axis=0)
            diag_own = jnp.tril(jnp.linalg.cholesky(jnp.where(is_owner, diag_blk, eye_blk)))
            diag_fac = lax.psum(jnp.where(is_owner, diag_own, 0.0), "row")
            diag_fac = jnp.where(own_col, diag_fac, eye_blk)
            solved = lax.linalg.triangular_solve(diag_fac, col_blk, left_side=False, lower=True, transpose_a=True)
            row_ids = (row_skip + jnp.arange(win_rblk)) * row_devs + row_id
            below_mask = (row_ids > step_idx)[:, None, None]
            on_diag = (row_ids == step_idx)[:, None, None]
            solved_blocks = solved.reshape(win_rblk, blk_size, blk_size)
            prior_col = col_blk.reshape(win_rblk, blk_size, blk_size)
            new_col = jnp.where(below_mask, solved_blocks, jnp.where(on_diag, diag_fac[None], prior_col))
            new_col = jnp.where(own_col, new_col, prior_col).reshape(win_rows, blk_size)
            window = lax.dynamic_update_slice_in_dim(window, new_col, col_off, axis=1)
            row_panel = lax.psum(jnp.where(below_mask & own_col, solved_blocks, 0.0).astype(jnp.bfloat16), "col")
            col_panel = transposed_panel(row_panel, row_id, col_id, row_devs, col_devs, row_skip, col_skip)
            update = lax.dot_general(row_panel.reshape(win_rows, blk_size), col_panel.reshape(win_cols, blk_size), (((1,), (1,)), ((), ())), preferred_element_type=jnp.float32)
            return window - update

        work_mat = a_loc.reshape(row_blocks * blk_size, local_cols)
        phase_count = min(blk_count, 8)
        bounds = [(phase_idx * blk_count) // phase_count for phase_idx in range(phase_count + 1)]
        for phase_idx in range(phase_count):
            row_start = (bounds[phase_idx] // row_devs) * blk_size
            col_start = (bounds[phase_idx] // col_devs) * blk_size
            window = lax.fori_loop(bounds[phase_idx], bounds[phase_idx + 1], panel_step, work_mat[row_start:, col_start:])
            work_mat = lax.dynamic_update_slice(work_mat, window, (row_start, col_start))
        row_blk_ids = jnp.arange(row_blocks) * row_devs + row_id
        col_blk_ids = jnp.arange(col_blocks) * col_devs + col_id
        keep_mask = row_blk_ids[:, None, None, None] >= col_blk_ids[None, None, :, None]
        factor = jnp.where(keep_mask, work_mat.reshape(row_blocks, blk_size, col_blocks, blk_size), 0.0)
        return factor.reshape(row_blocks, blk_size, local_cols)

    blk_spec = P(("batch", "row"), None, "col")
    return jax.shard_map(factor_local, mesh=mesh, in_specs=(blk_spec,), out_specs=blk_spec, check_vma=False)
```

profile of v0, /device:TPU:103, one launch (start us, length us, event | category | flops | bytes accessed | tf_op | source)
XLA Modules:
  0.0 6833.6 jit_solution(1120903417375208848)
XLA Ops:
  16.4 915.1 %while.185 = (s32[]{:T(128)}, f32[2048,1024]{0,1:T(8,128)}, s32[]{:T(128)}, s32[]{:T(128)}, pred[]{:T(512)}, /*index=5*/s32[]{:T(128)}, s32[]{:T(128)}, s32[]{:T...) while((s32[]{:T(128)}, f32[2048,1024]{0,1:T(8,128)}, ...), condition=%wide.region_8.10_spmd.clone.clone, body=%wide.region_0.9_spmd.clone.clone.sunk | while | flops 2341552640 | bytes 111692800 | solution.py:78
  938.0 905.5 %while.187 = (s32[]{:T(128)}, f32[1792,1024]{0,1:T(8,128)}, s32[]{:T(128)}, s32[]{:T(128)}, pred[]{:T(512)}, /*index=5*/s32[]{:T(128)}, s32[]{:T(128)}, s32[]{:T...) while((s32[]{:T(128)}, f32[1792,1024]{0,1:T(8,128)}, ...), condition=%wide.region_13.15_spmd.clone.clone, body=%wide.region_9.14_spmd.clone.clone.sunk | while | flops 2055389568 | bytes 101729432 | solution.py:78
  1853.3 874.2 %while.189 = (s32[]{:T(128)}, f32[1536,768]{0,1:T(8,128)}, s32[]{:T(128)}, s32[]{:T(128)}, pred[]{:T(512)}, /*index=5*/s32[]{:T(128)}, s32[]{:T(128)}, s32[]{:T(...) while((s32[]{:T(128)}, f32[1536,768]{0,1:T(8,128)}, ...), condition=%wide.region_18.20_spmd.clone.clone, body=%wide.region_14.19_spmd.clone.clone.sunk | while | flops 1567375744 | bytes 77741232 | solution.py:78
  1969.5 49.8 all-reduce.44.cloned.1.call-done
  2184.7 49.8 all-reduce.44.cloned.1.call-done
  2400.0 49.8 all-reduce.44.cloned.1.call-done
  2615.2 49.8 all-reduce.44.cloned.1.call-done
  2734.8 864.0 %while.191 = (s32[]{:T(128)}, f32[1280,768]{0,1:T(8,128)}, s32[]{:T(128)}, s32[]{:T(128)}, pred[]{:T(512)}, /*index=5*/s32[]{:T(128)}, s32[]{:T(128)}, s32[]{:T(...) while((s32[]{:T(128)}, f32[1280,768]{0,1:T(8,128)}, ...), condition=%wide.region_23.25_spmd.clone.clone, body=%wide.region_19.24_spmd.clone.clone.sunk | while | flops 1314832768 | bytes 72496304 | solution.py:78
  2849.1 51.1 all-reduce.50.cloned.1.call-done
  3062.4 50.2 all-reduce.50.cloned.1.call-done
  3275.1 50.8 all-reduce.50.cloned.1.call-done
  3489.1 49.2 all-reduce.50.cloned.1.call-done
  3603.6 823.7 %while.193 = (s32[]{:T(128)}, f32[1024,512]{0,1:T(8,128)S(1)}, s32[]{:T(128)}, s32[]{:T(128)}, pred[]{:T(512)}, /*index=5*/s32[]{:T(128)}, s32[]{:T(128)}, s32[]...) while((s32[]{:T(128)}, f32[1024,512]{0,1:T(8,128)S(1)}, ...), condition=%wide.region_28.30_spmd.clone.clone, body=%wide.region_24.29_spmd.clone.clone.sunk | while | flops 927678848 | bytes 46935180 | solution.py:78
  3713.0 53.6 all-reduce.56.cloned.1.call-done
  3918.7 53.6 all-reduce.56.cloned.1.call-done
  4124.5 53.6 all-reduce.56.cloned.1.call-done
  4330.3 53.6 all-reduce.56.cloned.1.call-done
  4430.0 810.4 %while.195 = (s32[]{:T(128)}, f32[768,512]{0,1:T(8,128)}, s32[]{:T(128)}, s32[]{:T(128)}, pred[]{:T(512)}, /*index=5*/s32[]{:T(128)}, s32[]{:T(128)}, s32[]{:T(1...) while((s32[]{:T(128)}, f32[768,512]{0,1:T(8,128)}, ...), condition=%wide.region_33.35_spmd.clone.clone, body=%wide.region_29.34_spmd.clone.clone.sunk | while | flops 708755776 | bytes 46933188 | solution.py:78
  4541.6 51.1 all-reduce.62.cloned.1.call-done
  4744.7 50.1 all-reduce.62.cloned.1.call-done
  4946.9 50.8 all-reduce.62.cloned.1.call-done
  5150.8 49.1 all-reduce.62.cloned.1.call-done
  5244.1 783.3 %while.197 = (s32[]{:T(128)}, f32[512,256]{0,1:T(8,128)S(1)}, s32[]{:T(128)}, s32[]{:T(128)}, pred[]{:T(512)}, /*index=5*/s32[]{:T(128)}, s32[]{:T(128)}, s32[]{...) while((s32[]{:T(128)}, f32[512,256]{0,1:T(8,128)S(1)}, ...), condition=%wide.region_38.40_spmd.clone.clone, body=%wide.region_34.39_spmd.clone.clone.sunk | while | flops 422461728 | bytes 19798952 | solution.py:78
  5345.4 56.2 all-reduce.68.cloned.1.call-done
  5541.2 56.2 all-reduce.68.cloned.1.call-done
  5737.0 56.2 all-reduce.68.cloned.1.call-done
  5932.8 56.2 all-reduce.68.cloned.1.call-done
  6028.3 779.5 %while.199 = (s32[]{:T(128)}, f32[256,256]{0,1:T(8,128)S(1)}, s32[]{:T(128)}, s32[1]{0:T(128)}, s32[]{:T(128)}, /*index=5*/pred[]{:T(512)}, s32[]{:T(128)}, s32[...) while((s32[]{:T(128)}, f32[256,256]{0,1:T(8,128)S(1)}, ...), condition=%wide.region_43.45_spmd.clone.clone, body=%wide.region_39.44_spmd.clone.clone.sunk | while | flops 237355296 | bytes 12847859 | solution.py:78
  6128.7 56.8 all-reduce.74.cloned.1.call-done
  6324.0 55.9 all-reduce.74.cloned.1.call-done
  6518.6 56.5 all-reduce.74.cloned.1.call-done
  6714.6 54.9 all-reduce.74.cloned.1.call-done
  (2137 shorter events, 5584.3 us)
Async XLA Ops:
  55.8 130.3 %all-reduce.32.cloned.1.call-start = ((), (), s32[]{:S(2)}) async-start(), calls=%async_computation.1 | async-start | bytes 2097152 | tf_op jit(solution)/shard_map/while/body/eval_jaxpr/psum | solution.py:67
  281.2 130.2 %all-reduce.32.cloned.1.call-start = ((), (), s32[]{:S(2)}) async-start(), calls=%async_computation.1 | async-start | bytes 2097152 | tf_op jit(solution)/shard_map/while/body/eval_jaxpr/psum | solution.py:67
  506.3 130.3 %all-reduce.32.cloned.1.call-start = ((), (), s32[]{:S(2)}) async-start(), calls=%async_computation.1 | async-start | bytes 2097152 | tf_op jit(solution)/shard_map/while/body/eval_jaxpr/psum | solution.py:67
  731.7 130.3 %all-reduce.32.cloned.1.call-start = ((), (), s32[]{:S(2)}) async-start(), calls=%async_computation.1 | async-start | bytes 2097152 | tf_op jit(solution)/shard_map/while/body/eval_jaxpr/psum | solution.py:67
  977.3 129.8 %all-reduce.38.cloned.1.call-start = ((), (), s32[]{:S(2)}) async-start(), calls=%async_computation.4 | async-start | bytes 1835008 | tf_op jit(solution)/shard_map/while/body/eval_jaxpr/psum | solution.py:67
  1200.7 128.9 %all-reduce.38.cloned.1.call-start = ((), (), s32[]{:S(2)}) async-start(), calls=%async_computation.4 | async-start | bytes 1835008 | tf_op jit(solution)/shard_map/while/body/eval_jaxpr/psum | solution.py:67
  1423.2 129.5 %all-reduce.38.cloned.1.call-start = ((), (), s32[]{:S(2)}) async-start(), calls=%async_computation.4 | async-start | bytes 1835008 | tf_op jit(solution)/shard_map/while/body/eval_jaxpr/psum | solution.py:67
  1646.3 128.9 %all-reduce.38.cloned.1.call-start = ((), (), s32[]{:S(2)}) async-start(), calls=%async_computation.4 | async-start | bytes 1835008 | tf_op jit(solution)/shard_map/while/body/eval_jaxpr/psum | solution.py:67
  1892.7 126.5 %all-reduce.44.cloned.1.call-start = ((), (), s32[]{:S(2)}) async-start(), calls=%async_computation.7 | async-start | bytes 1572864 | tf_op jit(solution)/shard_map/while/body/eval_jaxpr/psum | solution.py:67
  2108.0 126.5 %all-reduce.44.cloned.1.call-start = ((), (), s32[]{:S(2)}) async-start(), calls=%async_computation.7 | async-start | bytes 1572864 | tf_op jit(solution)/shard_map/while/body/eval_jaxpr/psum | solution.py:67
  2323.2 126.5 %all-reduce.44.cloned.1.call-start = ((), (), s32[]{:S(2)}) async-start(), calls=%async_computation.7 | async-start | bytes 1572864 | tf_op jit(solution)/shard_map/while/body/eval_jaxpr/psum | solution.py:67
  2538.5 126.5 %all-reduce.44.cloned.1.call-start = ((), (), s32[]{:S(2)}) async-start(), calls=%async_computation.7 | async-start | bytes 1572864 | tf_op jit(solution)/shard_map/while/body/eval_jaxpr/psum | solution.py:67
  2774.2 126.0 %all-reduce.50.cloned.1.call-start = ((), (), s32[]{:S(2)}) async-start(), calls=%async_computation.10 | async-start | bytes 1310720 | tf_op jit(solution)/shard_map/while/body/eval_jaxpr/psum | solution.py:67
  2987.6 125.0 %all-reduce.50.cloned.1.call-start = ((), (), s32[]{:S(2)}) async-start(), calls=%async_computation.10 | async-start | bytes 1310720 | tf_op jit(solution)/shard_map/while/body/eval_jaxpr/psum | solution.py:67
  3200.2 125.7 %all-reduce.50.cloned.1.call-start = ((), (), s32[]{:S(2)}) async-start(), calls=%async_computation.10 | async-start | bytes 1310720 | tf_op jit(solution)/shard_map/while/body/eval_jaxpr/psum | solution.py:67
  3413.3 125.0 %all-reduce.50.cloned.1.call-start = ((), (), s32[]{:S(2)}) async-start(), calls=%async_computation.10 | async-start | bytes 1310720 | tf_op jit(solution)/shard_map/while/body/eval_jaxpr/psum | solution.py:67
  3641.1 125.5 %all-reduce.56.cloned.1.call-start = ((), (), s32[]{:S(2)}) async-start(), calls=%async_computation.13 | async-start | bytes 1048576 | tf_op jit(solution)/shard_map/while/body/eval_jaxpr/psum | solution.py:67
  3846.8 125.5 %all-reduce.56.cloned.1.call-start = ((), (), s32[]{:S(2)}) async-start(), calls=%async_computation.13 | async-start | bytes 1048576 | tf_op jit(solution)/shard_map/while/body/eval_jaxpr/psum | solution.py:67
  4052.7 125.4 %all-reduce.56.cloned.1.call-start = ((), (), s32[]{:S(2)}) async-start(), calls=%async_computation.13 | async-start | bytes 1048576 | tf_op jit(solution)/shard_map/while/body/eval_jaxpr/psum | solution.py:67
  4258.5 125.5 %all-reduce.56.cloned.1.call-start = ((), (), s32[]{:S(2)}) async-start(), calls=%async_computation.13 | async-start | bytes 1048576 | tf_op jit(solution)/shard_map/while/body/eval_jaxpr/psum | solution.py:67
  4469.4 123.4 %all-reduce.62.cloned.1.call-start = ((), (), s32[]{:S(2)}) async-start(), calls=%async_computation.16 | async-start | bytes 786432 | tf_op jit(solution)/shard_map/while/body/eval_jaxpr/psum | solution.py:67
  4672.4 122.4 %all-reduce.62.cloned.1.call-start = ((), (), s32[]{:S(2)}) async-start(), calls=%async_computation.16 | async-start | bytes 786432 | tf_op jit(solution)/shard_map/while/body/eval_jaxpr/psum | solution.py:67
  4874.6 123.1 %all-reduce.62.cloned.1.call-start = ((), (), s32[]{:S(2)}) async-start(), calls=%async_computation.16 | async-start | bytes 786432 | tf_op jit(solution)/shard_map/while/body/eval_jaxpr/psum | solution.py:67
  5077.5 122.4 %all-reduce.62.cloned.1.call-start = ((), (), s32[]{:S(2)}) async-start(), calls=%async_computation.16 | async-start | bytes 786432 | tf_op jit(solution)/shard_map/while/body/eval_jaxpr/psum | solution.py:67
  5281.4 120.2 %all-reduce.68.cloned.1.call-start = ((), (), s32[]{:S(2)}) async-start(), calls=%async_computation.19 | async-start | bytes 524288 | tf_op jit(solution)/shard_map/while/body/eval_jaxpr/psum | solution.py:67
  5477.3 120.1 %all-reduce.68.cloned.1.call-start = ((), (), s32[]{:S(2)}) async-start(), calls=%async_computation.19 | async-start | bytes 524288 | tf_op jit(solution)/shard_map/while/body/eval_jaxpr/psum | solution.py:67
  5673.1 120.1 %all-reduce.68.cloned.1.call-start = ((), (), s32[]{:S(2)}) async-start(), calls=%async_computation.19 | async-start | bytes 524288 | tf_op jit(solution)/shard_map/while/body/eval_jaxpr/psum | solution.py:67
  5868.9 120.1 %all-reduce.68.cloned.1.call-start = ((), (), s32[]{:S(2)}) async-start(), calls=%async_computation.19 | async-start | bytes 524288 | tf_op jit(solution)/shard_map/while/body/eval_jaxpr/psum | solution.py:67
  6065.5 119.9 %all-reduce.74.cloned.1.call-start = ((), (), s32[]{:S(2)}) async-start(), calls=%async_computation.22 | async-start | bytes 262144 | tf_op jit(solution)/shard_map/while/body/eval_jaxpr/psum | solution.py:67
  6260.9 119.0 %all-reduce.74.cloned.1.call-start = ((), (), s32[]{:S(2)}) async-start(), calls=%async_computation.22 | async-start | bytes 262144 | tf_op jit(solution)/shard_map/while/body/eval_jaxpr/psum | solution.py:67
  6455.5 119.6 %all-reduce.74.cloned.1.call-start = ((), (), s32[]{:S(2)}) async-start(), calls=%async_computation.22 | async-start | bytes 262144 | tf_op jit(solution)/shard_map/while/body/eval_jaxpr/psum | solution.py:67
  6650.5 119.0 %all-reduce.74.cloned.1.call-start = ((), (), s32[]{:S(2)}) async-start(), calls=%async_computation.22 | async-start | bytes 262144 | tf_op jit(solution)/shard_map/while/body/eval_jaxpr/psum | solution.py:67
  (116 other events, 7390.0 us)
Sparse Core Ops, SparseCore 0:
  127.3 58.7 all-reduce.31
  352.7 58.6 all-reduce.31
  577.8 58.7 all-reduce.31
  803.2 58.7 all-reduce.31
  1047.8 59.2 all-reduce.37
  1271.2 58.3 all-reduce.37
  1493.6 58.9 all-reduce.37
  1717.8 57.3 all-reduce.37
  1961.3 57.8 all-reduce.43
  2176.6 57.9 all-reduce.43
  2391.8 57.9 all-reduce.43
  2607.1 57.9 all-reduce.43
  2841.7 58.4 all-reduce.49
  3055.0 57.5 all-reduce.49
  3267.7 58.1 all-reduce.49
  3481.7 56.5 all-reduce.49
  3709.6 56.9 all-reduce.55
  3915.3 56.9 all-reduce.55
  4121.1 56.9 all-reduce.55
  4327.0 56.9 all-reduce.55
  4535.0 57.6 all-reduce.61
  4738.1 56.6 all-reduce.61
  4940.3 57.3 all-reduce.61
  5144.2 55.6 all-reduce.61
  5345.4 56.1 all-reduce.67
  5541.2 56.1 all-reduce.67
  5737.0 56.1 all-reduce.67
  5932.8 56.1 all-reduce.67
  6128.7 56.6 all-reduce.73
  6324.1 55.7 all-reduce.73
  6518.6 56.3 all-reduce.73
  6714.6 54.8 all-reduce.73
  (64 shorter events, 2316.6 us)
where the time goes:
time: 6860 us; the launch traced here: 6830 us
  waiting for transfers between devices  3840 us (56%)
  other arithmetic  1980 us (29%)
  local copies, waits for them, and re-layouts  643 us (9%)
  matrix products  251 us (4%)
  loops' own time  106 us (2%)
    psum x32, waiting for transfers between devices, panel_step(): lax.psum(jnp.where(below_mask & own_col, solved_blocks, 0.0).astype(jnp.b...  1640 us
    psum x32, waiting for transfers between devices, panel_step(): diag_fac = lax.psum(jnp.where(is_owner, diag_own, 0.0), 'row')  1190 us
    another operation x192, other arithmetic, panel_step(): jnp.linalg.cholesky(jnp.where(is_owner, diag_blk, eye_blk))  1090 us
    psum x32, waiting for transfers between devices, transposed_panel(): return lax.psum(spread, 'row')  1010 us
    another operation x124, other arithmetic, panel_step(): lax.linalg.triangular_solve(diag_fac, col_blk, left_side=False, lower=Tru...  650 us
    while x164, local copies, waits for them, and re-layouts  276 us
  transfers between devices with their start and end apart: 96, of which 96 were waited for; matrix products, arithmetic and copies ran while one was open for 5% of the time, Pallas kernels for 0%

commit v1 on v0

v1 whole, which is shorter than its diff:
```python
import functools

import jax
import jax.numpy as jnp
from jax import lax
from jax.experimental import pallas as pl
from jax.experimental.pallas import tpu as pltpu
from jax.sharding import PartitionSpec as P

F32 = jnp.float32
BF16 = jnp.bfloat16
MESH = pl.DeviceIdType.MESH
SUB = 8
LANE = 128
BASE = 16


def sub_bcast(x, q):
    return jnp.broadcast_to(x[q : q + 1, :], (SUB, LANE))


def lane_bcast(x, lane):
    return jnp.take_along_axis(x, jnp.full((SUB, LANE), lane, jnp.int32), axis=1)


def split3(x):
    high = x.astype(BF16)
    rest = x - high.astype(F32)
    mid = rest.astype(BF16)
    return high, mid, (rest - mid.astype(F32)).astype(BF16)


def swap_rows(x, bit, row_id):
    if bit == SUB // 2:
        return pltpu.roll(x, bit, 0)
    return jnp.where((row_id & bit) == 0, pltpu.roll(x, SUB - bit, 0), pltpu.roll(x, bit, 0))


def stack_sums(parts):
    row_id = lax.broadcasted_iota(jnp.int32, (SUB, LANE), 0)
    for bit in (4, 2, 1):
        low = (row_id & bit) == 0
        half = len(parts) // 2
        parts = [
            jnp.where(low, parts[n], parts[n + half]) + swap_rows(jnp.where(low, parts[n + half], parts[n]), bit, row_id)
            for n in range(half)
        ]
    return parts[0]


def eliminate(rows, lane0):
    row_id = lax.broadcasted_iota(jnp.int32, (SUB, LANE), 0)
    rows = [list(rows[0]), list(rows[1])]
    cols = [
        [lane_bcast(rows[0][0], lane0 + j) for j in range(SUB)],
        [lane_bcast(rows[1][0], lane0 + j) for j in range(BASE)],
    ]
    scale = [jnp.zeros((SUB, LANE), F32), jnp.zeros((SUB, LANE), F32)]
    pivot = sub_bcast(cols[0][0], 0)
    for j in range(BASE):
        t, q = divmod(j, SUB)
        inv = lax.rsqrt(pivot)
        scale[t] = jnp.where(row_id == q, inv, scale[t])
        if j + 1 < BASE:
            tn, qn = divmod(j + 1, SUB)
            near = sub_bcast(cols[tn][j], qn) * inv
            pivot = sub_bcast(cols[tn][j + 1], qn) - near * near
        below = cols[1][j] * inv
        here = cols[0][j] * inv if t == 0 else None
        for n in range(j + 1, BASE):
            tn, qn = divmod(n, SUB)
            other = sub_bcast(cols[tn][j], qn) * inv
            if t == 0 and tn == 0:
                cols[0][n] = cols[0][n] - here * other
            cols[1][n] = cols[1][n] - below * other
        masked = jnp.where(row_id > q, here if t == 0 else below, 0.0)
        for v in range(len(rows[0])):
            pivot_row = sub_bcast(rows[t][v], q) * inv
            rows[t][v] = rows[t][v] - masked * pivot_row
            if t == 0:
                rows[1][v] = rows[1][v] - below * pivot_row
    return [[x * scale[t] for x in rows[t]] for t in range(2)]


def factor_block(work, winv, prev):
    size = work.shape[1]
    prev[...] = jnp.zeros(prev.shape, F32)
    for half in range(size // LANE):
        views = [(work, 0), (work, 1), (winv, 0)] if half == 0 else [(work, 1), (winv, 0), (winv, 1)]
        first = half * LANE
        if half == 1:
            mid_part, inv_part = prev[:, LANE : 2 * LANE], prev[:, 2 * LANE :]
            prev[:, :LANE] = mid_part
            prev[:, LANE : 2 * LANE] = inv_part
            prev[:, 2 * LANE :] = jnp.zeros((BASE, LANE), F32)

        def body(s, carry, views=views, first=first):
            lane0 = s * BASE
            row0 = pl.multiple_of(first + lane0, BASE)

            def rows_at(row, t):
                return pl.ds(pl.multiple_of(row + SUB * t, SUB), SUB)

            rows = [[ref[rows_at(row0, t), LANE * g : LANE * (g + 1)] for ref, g in views] for t in range(2)]
            hi, mid, lo = split3(prev[...])
            lane = lax.broadcasted_iota(jnp.int32, (BASE, size - first), 1) + first
            after = lane >= row0 + BASE
            lhi, lmid, llo = [jnp.where(after, x[:, : size - first], jnp.zeros((), BF16)) for x in (hi, mid, lo)]
            update = lax.dot_general(
                jnp.concatenate([lhi, lhi, lmid, lhi, llo, lmid], axis=0),
                jnp.concatenate([hi, mid, hi, lo, hi, mid], axis=0),
                (((0,), (0,)), ((), ())),
                preferred_element_type=F32,
            )
            for v, (ref, g) in enumerate(views):
                ref[first:size, LANE * g : LANE * (g + 1)] -= update[:, LANE * v : LANE * (v + 1)]
            done = eliminate(rows, lane0)
            for t in range(2):
                for v, (ref, g) in enumerate(views):
                    ref[rows_at(row0, t), LANE * g : LANE * (g + 1)] = done[t][v]
                    prev[SUB * t : SUB * (t + 1), LANE * v : LANE * (v + 1)] = done[t][v]
            if first == 0:
                source = [jnp.where(s == LANE // BASE - 1, done[t][1], done[t][0]) for t in range(2)]
            else:
                source = [done[t][0] for t in range(2)]
            next_lane = (lane0 + BASE) % LANE
            for t in range(2):
                factor = [[lane_bcast(source[m], next_lane + SUB * t + n) for n in range(SUB)] for m in range(2)]
                for v, (ref, g) in enumerate(views):
                    parts = [factor[0][n] * done[0][v] + factor[1][n] * done[1][v] for n in range(SUB)]
                    ref[rows_at(row0 + BASE, t), LANE * g : LANE * (g + 1)] -= stack_sums(parts)
            return carry

        lax.fori_loop(0, LANE // BASE, body, 0)


def kernel(n_row, n_col, batch_axis, a_ref, o_ref, share, diag, panel, work, winv, prev, load_sem, store_sem, seed_send, seed_recv,
           send_sem, recv_sem):
    row_blocks, size, local_cols = a_ref.shape
    col_blocks = local_cols // size
    ratio = n_col // n_row
    steps = row_blocks * n_row
    batch = lax.axis_index(batch_axis)
    row = lax.axis_index("row")
    col = lax.axis_index("col")
    on_diag = lax.rem(col, n_row) == row
    row_slots = n_row * (row_blocks * (row_blocks + 1) // 2)

    def at(dev_row, dev_col):
        return (batch, dev_row, dev_col)

    def row_slot(k, a):
        g = k // n_row
        return n_row * (row_blocks * g - (g * (g - 1)) // 2) + (k - g * n_row) * (row_blocks - g) + a - g

    def col_slot(k, b):
        h = k // n_col
        return row_slots + n_col * (col_blocks * h - (h * (h - 1)) // 2) + (k - h * n_col) * (col_blocks - h) + b - h

    def first_a(k):
        return (k + n_row - row) // n_row

    def first_b(k):
        return (k + n_col - col) // n_col

    def home(ref, a, b):
        return ref.at[a, :, pl.ds(pl.multiple_of(b * size, size), size)]

    def col_of(k, b):
        return jnp.where(on_diag, row_slot(k, ratio * b + col // n_row), col_slot(k, b))

    def arrived(slot):
        pltpu.make_async_remote_copy(
            src_ref=panel.at[slot], dst_ref=panel.at[slot], send_sem=send_sem.at[0], recv_sem=recv_sem.at[slot],
            device_id=at(row, col), device_id_type=MESH,
        ).wait_recv()

    for a in range(row_blocks):
        for b in range(col_blocks):
            pltpu.make_async_copy(home(a_ref, a, b), share.at[a * col_blocks + b], load_sem).start()

    barrier = pltpu.get_barrier_semaphore()
    n_dev = n_row * n_col

    def greet(n, carry):
        other = lax.rem(row * n_col + col + n, n_dev)
        pl.semaphore_signal(barrier, inc=1, device_id=at(other // n_col, lax.rem(other, n_col)), device_id_type=MESH)
        return carry

    lax.fori_loop(1, n_dev, greet, 0)
    pl.semaphore_wait(barrier, n_dev - 1)
    pltpu.make_async_copy(share, share, load_sem).wait()

    def seed_copy(b, dev_row):
        block = (ratio * b + col // n_row) * col_blocks + b
        return pltpu.make_async_remote_copy(
            src_ref=share.at[block], dst_ref=diag.at[b], send_sem=seed_send.at[b, lax.rem(dev_row - row + n_row, n_row)],
            recv_sem=seed_recv.at[b], device_id=at(dev_row, col), device_id_type=MESH,
        )

    @pl.when(on_diag)
    def _():
        for b in range(col_blocks):
            for d in (1, n_row - 1, 2):
                seed_copy(b, lax.rem(row + d, n_row)).start()
        for b in range(col_blocks):
            diag[b] = share[(ratio * b + col // n_row) * col_blocks + b]

    def seed_arrived(b):
        @pl.when(jnp.logical_not(on_diag))
        def _():
            seed_copy(b, row).wait_recv()

    seed_arrived(0)

    def clear(n, carry):
        a, b = n // col_blocks, lax.rem(n, col_blocks)

        @pl.when(a * n_row + row < b * n_col + col)
        def _():
            share[n] = jnp.zeros((size, size), F32)
            pltpu.make_async_copy(share.at[n], home(o_ref, a, b), store_sem).start()

        return carry

    lax.fori_loop(0, row_blocks * col_blocks, clear, 0)

    def times_t(x, y):
        return lax.dot_general(x, y, (((1,), (1,)), ((), ())), preferred_element_type=F32)

    def send_block(k, a):
        i = a * n_row + row
        slot = row_slot(k, a)
        to_col, to_b = lax.rem(i, n_col), i // n_col
        for d in range(1, n_row):
            pltpu.make_async_remote_copy(
                src_ref=panel.at[slot], dst_ref=panel.at[col_slot(k, to_b)], send_sem=send_sem.at[a],
                recv_sem=recv_sem.at[col_slot(k, to_b)], device_id=at(lax.rem(row + d, n_row), to_col), device_id_type=MESH,
            ).start()
        for d in range(1, n_col):
            pltpu.make_async_remote_copy(
                src_ref=panel.at[slot], dst_ref=panel.at[slot], send_sem=send_sem.at[a], recv_sem=recv_sem.at[slot],
                device_id=at(row, lax.rem(col + d, n_col)), device_id_type=MESH,
            ).start()

    copies = n_row - 1 + n_col - 1

    def sends_done(k):
        def one(a, carry):
            every = panel.at[pl.ds(0, copies)]
            pltpu.make_async_copy(every, every, send_sem.at[a]).wait()
            return carry

        lax.fori_loop(first_a(k), row_blocks, one, 0)

    def step(k, carry):
        mine = col == lax.rem(k, n_col)
        kb = k // n_col

        @pl.when(mine)
        def _():
            work[0:size, :] = diag[kb]
            work[size:, :] = jnp.zeros((BASE, size), F32)
            r_id = lax.broadcasted_iota(jnp.int32, (size + BASE, size), 0)
            c_id = lax.broadcasted_iota(jnp.int32, (size + BASE, size), 1)
            winv[...] = jnp.where(r_id == c_id, 1.0, 0.0).astype(F32)
            factor_block(work, winv, prev)

            def solve(a, carry):
                n = a * col_blocks + kb

                @pl.when(k > 0)
                def _():
                    arrived(row_slot(k - 1, a))
                    share[n] -= times_t(panel[row_slot(k - 1, a)], panel[col_of(k - 1, kb)])

                x = lax.dot_general(
                    share[n], winv[0:size, :], (((1,), (1,)), ((), ())), precision=lax.Precision.HIGHEST,
                    preferred_element_type=F32,
                )
                panel[row_slot(k, a)] = x.astype(BF16)
                share[n] = x
                send_block(k, a)
                pltpu.make_async_copy(share.at[n], home(o_ref, a, kb), store_sem).start()
                return carry

            lax.fori_loop(first_a(k), row_blocks, solve, 0)

            @pl.when(row == lax.rem(k, n_row))
            def _():
                for d in range(1, n_row):
                    seed_copy(kb, lax.rem(row + d, n_row)).wait_send()
                r_id = lax.broadcasted_iota(jnp.int32, (size, size), 0)
                c_id = lax.broadcasted_iota(jnp.int32, (size, size), 1)
                n = (k // n_row) * col_blocks + kb
                share[n] = jnp.where(r_id >= c_id, work[0:size, :].T, 0.0)
                pltpu.make_async_copy(share.at[n], home(o_ref, k // n_row, kb), store_sem).start()

        @pl.when(k > 0)
        def _():
            p = k - 1
            owner = col == lax.rem(p, n_col)

            @pl.when(k == 1)
            def _():
                for b in range(1, col_blocks):
                    seed_arrived(b)

            @pl.when(jnp.logical_not(jnp.logical_or(owner, mine)))
            def _():
                lax.fori_loop(first_a(p), row_blocks, lambda a, c: (arrived(row_slot(p, a)), c)[1], 0)

            def column(b, carry):
                @pl.when(jnp.logical_not(on_diag))
                def _():
                    arrived(col_slot(p, b))

                other = col_of(p, b)
                diag[b] -= times_t(panel[other], panel[other])

                def block(a, carry):
                    share[a * col_blocks + b] -= times_t(panel[row_slot(p, a)], panel[other])
                    return carry

                lax.fori_loop(first_a(b * n_col + col), row_blocks, block, 0)
                return carry

            lax.fori_loop(jnp.where(mine, kb + 1, first_b(p)), col_blocks, column, 0)

        @pl.when(jnp.logical_and(col == lax.rem(k + 1, n_col), k + 1 < steps))
        def _():
            nb = (k + 1) // n_col
            slot = col_of(k, nb)
            arrived(slot)
            diag[nb] -= times_t(panel[slot], panel[slot])

        @pl.when(jnp.logical_and(k >= n_col // 2, col == lax.rem(k + n_col // 2, n_col)))
        def _():
            sends_done(k - n_col // 2)

        return carry

    lax.fori_loop(0, steps, step, 0)

    for m in range(n_col // 2):
        k = steps - n_col // 2 + m

        @pl.when(col == k % n_col)
        def _():
            sends_done(k)

    pltpu.make_async_copy(share, share, store_sem).wait()


def solution(mesh):
    n_row = mesh.shape["row"]
    n_col = mesh.shape["col"]

    def factor_local(a_loc):
        row_blocks, size, local_cols = a_loc.shape
        col_blocks = local_cols // size
        slots = n_row * (row_blocks * (row_blocks + 1) // 2) + n_col * (col_blocks * (col_blocks + 1) // 2)
        return pl.pallas_call(
            functools.partial(kernel, n_row, n_col, "batch"),
            out_shape=jax.ShapeDtypeStruct(a_loc.shape, F32),
            in_specs=[pl.BlockSpec(memory_space=pl.ANY)],
            out_specs=pl.BlockSpec(memory_space=pl.ANY),
            scratch_shapes=[
                pltpu.VMEM((row_blocks * col_blocks, size, size), F32),
                pltpu.VMEM((col_blocks, size, size), F32),
                pltpu.VMEM((slots, size, size), BF16),
                pltpu.VMEM((size + BASE, size), F32),
                pltpu.VMEM((size + BASE, size), F32),
                pltpu.VMEM((BASE, 3 * LANE), F32),
                pltpu.SemaphoreType.DMA,
                pltpu.SemaphoreType.DMA,
                pltpu.SemaphoreType.DMA((col_blocks, n_row)),
                pltpu.SemaphoreType.DMA((col_blocks,)),
                pltpu.SemaphoreType.DMA((row_blocks,)),
                pltpu.SemaphoreType.DMA((slots,)),
            ],
            compiler_params=pltpu.CompilerParams(
                collective_id=0, has_side_effects=True, vmem_limit_bytes=60 * 1024 * 1024
            ),
            name="cholesky",
        )(a_loc)

    blk_spec = P(("batch", "row"), None, "col")
    return jax.shard_map(factor_local, mesh=mesh, in_specs=(blk_spec,), out_specs=blk_spec, check_vma=False)
```

time: 6860 us -> 885 us (0.13)
  waiting for transfers between devices: 3840 us -> 0 us
  other arithmetic: 1980 us -> 0 us
  Pallas kernels: 0 us -> 877 us
  local copies, waits for them, and re-layouts: 643 us -> 8.44 us
  matrix products: 251 us -> 0 us
  loops' own time: 106 us -> 0 us
    psum x96 -> x0, waiting for transfers between devices: 3830 us -> none  [the longest x32 1640 us: panel_step(): lax.psum(jnp.where(below_mask & own_col, solved_blocks, 0.0).astype(jnp.b...]
    another operation x316 -> x0, other arithmetic: 1740 us -> none  [the longest x192 1090 us: panel_step(): jnp.linalg.cholesky(jnp.where(is_owner, diag_blk, eye_blk))]
    pallas_call x0 -> x1, Pallas kernels: none -> 877 us  [factor_local(): pl.pallas_call(functools.partial(kernel, n_row, n_col, 'batch'), out_shap...]
    while x164 -> x0, local copies, waits for them, and re-layouts: 276 us -> none
    select_n x113 -> x0, other arithmetic: 157 us -> none  [the longest x24 70.2 us: panel_step(): new_col = jnp.where(own_col, new_col, prior_col).reshape(win_rows, blk_size)]
    another operation x592 -> x0, local copies, waits for them, and re-layouts: 154 us -> none
    dot_general x32 -> x0, matrix products: 132 us -> none  [panel_step(): lax.dot_general(row_panel.reshape(win_rows, blk_size), col_panel.reshape(...]
    another operation x160 -> x0, matrix products: 119 us -> none  [the longest x96 104 us: panel_step(): lax.linalg.triangular_solve(diag_fac, col_blk, left_side=False, lower=Tru...]
  transfers between devices with their start and end apart: 96 -> 0, of which waited for: 96 -> 0; matrix products, arithmetic and copies ran while one was open for 5% -> 0% of each run, Pallas kernels for 0% -> 0%
where the time goes in v1:
time: 885 us
  Pallas kernels  877 us (99%)
    pallas_call x1, Pallas kernels, factor_local(): pl.pallas_call(functools.partial(kernel, n_row, n_col, 'batch'), out_shap...  877 us

profile of v1, /device:TPU:103, one launch (start us, length us, event | category | flops | bytes accessed | tf_op | source)
XLA Modules:
  0.0 885.0 jit_solution(7705551509036134026)
XLA Ops:
  0.0 876.5 %cholesky.1 = f32[8,256,1024]{2,1,0:T(8,128)} custom-call(f32[8,256,1024]{2,1,0:T(8,128)} %a_ref.1), custom_call_target="tpu_custom_call" | custom-call | tf_op jit(solution)/shard_map/cholesky/pallas_call | solution.py:363
  876.5 8.4 copy.3

commit v2 on v1

--- a/solution.py
+++ b/solution.py
@@ -135,14 +135,16 @@
 
 
 def kernel(n_row, n_col, batch_axis, a_ref, o_ref, share, diag, panel, work, winv, prev, load_sem, store_sem, seed_send, seed_recv,
-           send_sem, recv_sem):
+           send_sem, pass_sem, recv_sem):
     row_blocks, size, local_cols = a_ref.shape
     col_blocks = local_cols // size
     ratio = n_col // n_row
     steps = row_blocks * n_row
+    depth = pass_sem.shape[0]
     batch = lax.axis_index(batch_axis)
     row = lax.axis_index("row")
     col = lax.axis_index("col")
+    odd = lax.rem(col, 2)
     on_diag = lax.rem(col, n_row) == row
     row_slots = n_row * (row_blocks * (row_blocks + 1) // 2)
 
@@ -166,35 +168,119 @@
     def home(ref, a, b):
         return ref.at[a, :, pl.ds(pl.multiple_of(b * size, size), size)]
 
+    def spot(a, b):
+        return b * row_blocks + a
+
     def col_of(k, b):
         return jnp.where(on_diag, row_slot(k, ratio * b + col // n_row), col_slot(k, b))
 
+    def copy(src_slot, dst_slot, sem, device):
+        return pltpu.make_async_remote_copy(
+            src_ref=panel.at[src_slot], dst_ref=panel.at[dst_slot], send_sem=sem, recv_sem=recv_sem.at[dst_slot],
+            device_id=device, device_id_type=MESH,
+        )
+
     def arrived(slot):
-        pltpu.make_async_remote_copy(
-            src_ref=panel.at[slot], dst_ref=panel.at[slot], send_sem=send_sem.at[0], recv_sem=recv_sem.at[slot],
-            device_id=at(row, col), device_id_type=MESH,
-        ).wait_recv()
+        copy(slot, slot, send_sem.at[0, 0], at(row, col)).wait_recv()
+
+    def start(c):
+        c.start()
+
+    def finish(c):
+        c.wait_send()
+
+    def down_column(k, a, sems, target, act):
+        slot = row_slot(k, a)
+        dst = col_slot(k, (a * n_row + row) // n_col)
+        for m, d in enumerate((1, n_row - 1, 2)):
+            act(copy(slot, dst, sems[m], at(lax.rem(row + d, n_row), target)))
+
+    def source_sends(k, a, act):
+        ahead = a * n_row + row - k
+        slot = row_slot(k, a)
+
+        @pl.when(jnp.logical_or(ahead <= 2, lax.rem(ahead, n_col) == 0))
+        def _():
+            down_column(k, a, [send_sem.at[a, m] for m in range(3)], lax.rem(col + ahead, n_col), act)
+
+        @pl.when(jnp.logical_or(odd == 0, jnp.logical_or(ahead == 1, ahead >= n_col - 1)))
+        def _():
+            up = jnp.logical_or(odd == 0, ahead == 1)
+            act(copy(slot, slot, send_sem.at[a, 3], at(row, lax.rem(jnp.where(up, col + 1, col - 1), n_col))))
+
+        @pl.when(ahead >= 2)
+        def _():
+            act(copy(slot, slot, send_sem.at[a, 4], at(row, lax.rem(col - odd + 3, n_col))))
+
+        @pl.when(ahead >= n_col - 2 - odd)
+        def _():
+            act(copy(slot, slot, send_sem.at[a, 5], at(row, lax.rem(col - odd - 1 + n_col, n_col))))
+
+    def lead(p):
+        return lax.rem(col - lax.rem(p, n_col) + n_col, n_col)
+
+    def hops(p):
+        return lax.rem(col // 2 - lax.rem(p, n_col) // 2 + n_col // 2, n_col // 2)
+
+    def passes(p):
+        return jnp.logical_and(odd == 1, hops(p) != 0)
+
+    def first_passed(p):
+        low = jnp.where(passes(p), jnp.maximum(lead(p) - 1, 2), lead(p))
+        return (p + low - row + n_row - 1) // n_row
+
+    def pass_on(p, a, act):
+        i = a * n_row + row
+        ahead = i - p
+        slot = row_slot(p, a)
+        sems = pass_sem.at[lax.rem(p, depth), a]
+        src_odd = lax.rem(p, 2)
+        far = n_col - 2 - src_odd
+
+        @pl.when(passes(p))
+        def _():
+            h = hops(p)
+            via_prev = jnp.logical_and(lax.rem(a, 2) == 1, ahead >= far)
+            mine_to_pass = jnp.logical_or(
+                jnp.logical_and(h == 1, jnp.logical_not(via_prev)), jnp.logical_and(h == n_col // 2 - 1, via_prev)
+            )
+
+            @pl.when(jnp.logical_and(mine_to_pass, ahead >= n_col // 2 - src_odd))
+            def _():
+                act(copy(slot, slot, sems.at[4], at(row, lax.rem(jnp.where(h == 1, col + 2, col - 2 + n_col), n_col))))
+
+            act(copy(slot, slot, sems.at[3], at(row, col - 1)))
+
+        @pl.when(jnp.logical_and(lax.rem(i, n_col) == col, ahead >= 3))
+        def _():
+            down_column(p, a, [sems.at[m] for m in range(3)], col, act)
+
+    def receive(p, a):
+        arrived(row_slot(p, a))
+        pass_on(p, a, start)
+
+    def loop(lo, hi, fn):
+        lax.fori_loop(lo, hi, lambda n, c: (fn(n), c)[1], 0)
 
     for a in range(row_blocks):
         for b in range(col_blocks):
-            pltpu.make_async_copy(home(a_ref, a, b), share.at[a * col_blocks + b], load_sem).start()
+            pltpu.make_async_copy(home(a_ref, a, b), share.at[spot(a, b)], load_sem).start()
 
     barrier = pltpu.get_barrier_semaphore()
     n_dev = n_row * n_col
 
-    def greet(n, carry):
+    def greet(n):
         other = lax.rem(row * n_col + col + n, n_dev)
         pl.semaphore_signal(barrier, inc=1, device_id=at(other // n_col, lax.rem(other, n_col)), device_id_type=MESH)
-        return carry
-
-    lax.fori_loop(1, n_dev, greet, 0)
+
+    loop(1, n_dev, greet)
     pl.semaphore_wait(barrier, n_dev - 1)
     pltpu.make_async_copy(share, share, load_sem).wait()
 
     def seed_copy(b, dev_row):
-        block = (ratio * b + col // n_row) * col_blocks + b
         return pltpu.make_async_remote_copy(
-            src_ref=share.at[block], dst_ref=diag.at[b], send_sem=seed_send.at[b, lax.rem(dev_row - row + n_row, n_row)],
+            src_ref=share.at[spot(ratio * b + col // n_row, b)], dst_ref=diag.at[b],
+            send_sem=seed_send.at[b, lax.rem(dev_row - row + n_row, n_row)],
             recv_sem=seed_recv.at[b], device_id=at(dev_row, col), device_id_type=MESH,
         )
 
@@ -204,7 +290,7 @@
             for d in (1, n_row - 1, 2):
                 seed_copy(b, lax.rem(row + d, n_row)).start()
         for b in range(col_blocks):
-            diag[b] = share[(ratio * b + col // n_row) * col_blocks + b]
+            diag[b] = share[spot(ratio * b + col // n_row, b)]
 
     def seed_arrived(b):
         @pl.when(jnp.logical_not(on_diag))
@@ -213,49 +299,66 @@
 
     seed_arrived(0)
 
-    def clear(n, carry):
-        a, b = n // col_blocks, lax.rem(n, col_blocks)
+    def clear(n):
+        a, b = lax.rem(n, row_blocks), n // row_blocks
 
         @pl.when(a * n_row + row < b * n_col + col)
         def _():
             share[n] = jnp.zeros((size, size), F32)
             pltpu.make_async_copy(share.at[n], home(o_ref, a, b), store_sem).start()
 
-        return carry
-
-    lax.fori_loop(0, row_blocks * col_blocks, clear, 0)
+    loop(0, row_blocks * col_blocks, clear)
 
     def times_t(x, y):
         return lax.dot_general(x, y, (((1,), (1,)), ((), ())), preferred_element_type=F32)
 
-    def send_block(k, a):
-        i = a * n_row + row
-        slot = row_slot(k, a)
-        to_col, to_b = lax.rem(i, n_col), i // n_col
-        for d in range(1, n_row):
-            pltpu.make_async_remote_copy(
-                src_ref=panel.at[slot], dst_ref=panel.at[col_slot(k, to_b)], send_sem=send_sem.at[a],
-                recv_sem=recv_sem.at[col_slot(k, to_b)], device_id=at(lax.rem(row + d, n_row), to_col), device_id_type=MESH,
-            ).start()
-        for d in range(1, n_col):
-            pltpu.make_async_remote_copy(
-                src_ref=panel.at[slot], dst_ref=panel.at[slot], send_sem=send_sem.at[a], recv_sem=recv_sem.at[slot],
-                device_id=at(row, lax.rem(col + d, n_col)), device_id_type=MESH,
-            ).start()
-
-    copies = n_row - 1 + n_col - 1
-
-    def sends_done(k):
-        def one(a, carry):
-            every = panel.at[pl.ds(0, copies)]
-            pltpu.make_async_copy(every, every, send_sem.at[a]).wait()
-            return carry
-
-        lax.fori_loop(first_a(k), row_blocks, one, 0)
-
-    def step(k, carry):
+    def update_block(p, a, b):
+        share[spot(a, b)] -= times_t(panel[row_slot(p, a)], panel[col_of(p, b)])
+
+    def update_diag(p, b):
+        other = panel[col_of(p, b)]
+        diag[b] -= times_t(other, other)
+
+    def column_arrived(p, b):
+        @pl.when(jnp.logical_not(on_diag))
+        def _():
+            arrived(col_slot(p, b))
+
+    def trail(p, b_from):
+        def column(b):
+            column_arrived(p, b)
+            update_diag(p, b)
+            lo = first_a(b * n_col + col)
+            lone = lax.rem(row_blocks - lo, 2)
+
+            @pl.when(lone == 1)
+            def _():
+                update_block(p, lo, b)
+
+            def pair(m):
+                a = lo + lone + 2 * m
+                both = pl.ds(spot(a, b), 2)
+                left = panel[pl.ds(row_slot(p, a), 2)].reshape(2 * size, size)
+                share[both] -= times_t(left, panel[col_of(p, b)]).reshape(2, size, size)
+
+            loop(0, (row_blocks - lo) // 2, pair)
+
+        loop(b_from, col_blocks, column)
+
+    def step(k):
         mine = col == lax.rem(k, n_col)
         kb = k // n_col
+        last = k - 1
+        soon = jnp.logical_and(col == lax.rem(k + 1, n_col), k + 1 < steps)
+
+        @pl.when(jnp.logical_and(k > depth, lead(last - depth + n_col) != 0))
+        def _():
+            loop(first_passed(last - depth), row_blocks, lambda a: pass_on(last - depth, a, finish))
+
+        @pl.when(k == 1)
+        def _():
+            for b in range(1, col_blocks):
+                seed_arrived(b)
 
         @pl.when(mine)
         def _():
@@ -266,13 +369,17 @@
             winv[...] = jnp.where(r_id == c_id, 1.0, 0.0).astype(F32)
             factor_block(work, winv, prev)
 
-            def solve(a, carry):
-                n = a * col_blocks + kb
+            def solve(a):
+                n = spot(a, kb)
+
+                @pl.when(k > 1)
+                def _():
+                    update_block(k - 2, a, kb)
 
                 @pl.when(k > 0)
                 def _():
-                    arrived(row_slot(k - 1, a))
-                    share[n] -= times_t(panel[row_slot(k - 1, a)], panel[col_of(k - 1, kb)])
+                    receive(last, a)
+                    update_block(last, a, kb)
 
                 x = lax.dot_general(
                     share[n], winv[0:size, :], (((1,), (1,)), ((), ())), precision=lax.Precision.HIGHEST,
@@ -280,11 +387,10 @@
                 )
                 panel[row_slot(k, a)] = x.astype(BF16)
                 share[n] = x
-                send_block(k, a)
+                source_sends(k, a, start)
                 pltpu.make_async_copy(share.at[n], home(o_ref, a, kb), store_sem).start()
-                return carry
-
-            lax.fori_loop(first_a(k), row_blocks, solve, 0)
+
+            loop(first_a(k), row_blocks, solve)
 
             @pl.when(row == lax.rem(k, n_row))
             def _():
@@ -292,63 +398,59 @@
                     seed_copy(kb, lax.rem(row + d, n_row)).wait_send()
                 r_id = lax.broadcasted_iota(jnp.int32, (size, size), 0)
                 c_id = lax.broadcasted_iota(jnp.int32, (size, size), 1)
-                n = (k // n_row) * col_blocks + kb
+                n = spot(k // n_row, kb)
                 share[n] = jnp.where(r_id >= c_id, work[0:size, :].T, 0.0)
                 pltpu.make_async_copy(share.at[n], home(o_ref, k // n_row, kb), store_sem).start()
 
-        @pl.when(k > 0)
-        def _():
-            p = k - 1
-            owner = col == lax.rem(p, n_col)
-
-            @pl.when(k == 1)
-            def _():
-                for b in range(1, col_blocks):
-                    seed_arrived(b)
-
-            @pl.when(jnp.logical_not(jnp.logical_or(owner, mine)))
-            def _():
-                lax.fori_loop(first_a(p), row_blocks, lambda a, c: (arrived(row_slot(p, a)), c)[1], 0)
-
-            def column(b, carry):
-                @pl.when(jnp.logical_not(on_diag))
-                def _():
-                    arrived(col_slot(p, b))
-
-                other = col_of(p, b)
-                diag[b] -= times_t(panel[other], panel[other])
-
-                def block(a, carry):
-                    share[a * col_blocks + b] -= times_t(panel[row_slot(p, a)], panel[other])
-                    return carry
-
-                lax.fori_loop(first_a(b * n_col + col), row_blocks, block, 0)
-                return carry
-
-            lax.fori_loop(jnp.where(mine, kb + 1, first_b(p)), col_blocks, column, 0)
-
-        @pl.when(jnp.logical_and(col == lax.rem(k + 1, n_col), k + 1 < steps))
+            @pl.when(k > 1)
+            def _():
+                trail(k - 2, kb + 1)
+
+            @pl.when(k > 0)
+            def _():
+                trail(last, kb + 1)
+
+        @pl.when(jnp.logical_and(k > 0, jnp.logical_not(mine)))
+        def _():
+            @pl.when(col != lax.rem(last, n_col))
+            def _():
+                loop(first_passed(last), row_blocks, lambda a: receive(last, a))
+
+            @pl.when(jnp.logical_not(soon))
+            def _():
+                trail(last, first_b(last))
+
+        @pl.when(soon)
         def _():
             nb = (k + 1) // n_col
-            slot = col_of(k, nb)
-            arrived(slot)
-            diag[nb] -= times_t(panel[slot], panel[slot])
+
+            @pl.when(k > 0)
+            def _():
+                column_arrived(last, nb)
+                update_diag(last, nb)
+
+            arrived(col_of(k, nb))
+            update_diag(k, nb)
 
         @pl.when(jnp.logical_and(k >= n_col // 2, col == lax.rem(k + n_col // 2, n_col)))
         def _():
-            sends_done(k - n_col // 2)
-
-        return carry
-
-    lax.fori_loop(0, steps, step, 0)
-
-    for m in range(n_col // 2):
-        k = steps - n_col // 2 + m
-
-        @pl.when(col == k % n_col)
-        def _():
-            sends_done(k)
-
+            loop(first_a(k - n_col // 2), row_blocks, lambda a: source_sends(k - n_col // 2, a, finish))
+
+    loop(0, steps, step)
+
+    def last_passes(p):
+        @pl.when(lead(p) != 0)
+        def _():
+            loop(first_passed(p), row_blocks, lambda a: pass_on(p, a, finish))
+
+    loop(steps - 1 - depth, steps - 1, last_passes)
+
+    def last_sends(k):
+        @pl.when(col == lax.rem(k, n_col))
+        def _():
+            loop(first_a(k), row_blocks, lambda a: source_sends(k, a, finish))
+
+    loop(steps - n_col // 2, steps, last_sends)
     pltpu.make_async_copy(share, share, store_sem).wait()
 
 
@@ -376,7 +478,8 @@
                 pltpu.SemaphoreType.DMA,
                 pltpu.SemaphoreType.DMA((col_blocks, n_row)),
                 pltpu.SemaphoreType.DMA((col_blocks,)),
-                pltpu.SemaphoreType.DMA((row_blocks,)),
+                pltpu.SemaphoreType.DMA((row_blocks, 6)),
+                pltpu.SemaphoreType.DMA((4, row_blocks, 5)),
                 pltpu.SemaphoreType.DMA((slots,)),
             ],
             compiler_params=pltpu.CompilerParams(

time: 885 us -> 439 us (0.50)
  Pallas kernels: 877 us -> 430 us
    pallas_call x1, Pallas kernels: 877 us -> 430 us  [factor_local(): pl.pallas_call(functools.partial(kernel, n_row, n_col, 'batch'), out_shap...]
where the time goes in v2:
time: 439 us
  Pallas kernels  430 us (98%)
  local copies, waits for them, and re-layouts  8.44 us (2%)
    pallas_call x1, Pallas kernels, factor_local(): pl.pallas_call(functools.partial(kernel, n_row, n_col, 'batch'), out_shap...  430 us

profile of v2, /device:TPU:103, one launch (start us, length us, event | category | flops | bytes accessed | tf_op | source)
XLA Modules:
  0.0 438.9 jit_solution(11797093552698946116)
XLA Ops:
  0.0 430.5 %cholesky.1 = f32[8,256,1024]{2,1,0:T(8,128)} custom-call(f32[8,256,1024]{2,1,0:T(8,128)} %a_ref.1), custom_call_target="tpu_custom_call" | custom-call | tf_op jit(solution)/shard_map/cholesky/pallas_call | solution.py:465
  430.5 8.4 %copy.3 = f32[8,256,1024]{2,1,0:T(8,128)} copy(f32[8,256,1024]{2,1,0:T(8,128)} %cholesky.1) | data formatting | bytes 16777216

commit v3 on v2

--- a/solution.py
+++ b/solution.py
@@ -134,7 +134,7 @@
         lax.fori_loop(0, LANE // BASE, body, 0)
 
 
-def kernel(n_row, n_col, batch_axis, a_ref, o_ref, share, diag, panel, work, winv, prev, load_sem, store_sem, seed_send, seed_recv,
+def kernel(n_row, n_col, batch_axis, a_ref, o_ref, share, diag, panel, work, winv, winv3, prev, load_sem, store_sem, seed_send, seed_recv,
            send_sem, pass_sem, recv_sem):
     row_blocks, size, local_cols = a_ref.shape
     col_blocks = local_cols // size
@@ -189,19 +189,24 @@
     def finish(c):
         c.wait_send()
 
-    def down_column(k, a, sems, target, act):
+    def down_column(k, a, ways, sems, target, act):
         slot = row_slot(k, a)
         dst = col_slot(k, (a * n_row + row) // n_col)
-        for m, d in enumerate((1, n_row - 1, 2)):
+        for m, d in enumerate(ways):
             act(copy(slot, dst, sems[m], at(lax.rem(row + d, n_row), target)))
 
     def source_sends(k, a, act):
         ahead = a * n_row + row - k
         slot = row_slot(k, a)
 
-        @pl.when(jnp.logical_or(ahead <= 2, lax.rem(ahead, n_col) == 0))
-        def _():
-            down_column(k, a, [send_sem.at[a, m] for m in range(3)], lax.rem(col + ahead, n_col), act)
+        @pl.when(ahead == 1)
+        def _():
+            dst = col_slot(k, (k + 1) // n_col)
+            act(copy(slot, dst, send_sem.at[a, 0], at(lax.rem(row + 1, n_row), lax.rem(col + 1, n_col))))
+
+        @pl.when(lax.rem(ahead, n_col) == 0)
+        def _():
+            down_column(k, a, (1, n_row - 1, 2), [send_sem.at[a, m] for m in range(3)], col, act)
 
         @pl.when(jnp.logical_or(odd == 0, jnp.logical_or(ahead == 1, ahead >= n_col - 1)))
         def _():
@@ -251,9 +256,20 @@
 
             act(copy(slot, slot, sems.at[3], at(row, col - 1)))
 
-        @pl.when(jnp.logical_and(lax.rem(i, n_col) == col, ahead >= 3))
-        def _():
-            down_column(p, a, [sems.at[m] for m in range(3)], col, act)
+        own = lax.rem(i, n_col) == col
+
+        @pl.when(jnp.logical_and(own, ahead == 1))
+        def _():
+            down_column(p, a, (n_row - 1, 2), [sems.at[m] for m in range(2)], col, act)
+
+        @pl.when(jnp.logical_and(own, ahead > 1))
+        def _():
+            down_column(p, a, (1, n_row - 1, 2), [sems.at[m] for m in range(3)], col, act)
+
+    def passed(p):
+        @pl.when(lead(p) != 0)
+        def _():
+            loop(first_passed(p), row_blocks, lambda a: pass_on(p, a, finish))
 
     def receive(p, a):
         arrived(row_slot(p, a))
@@ -345,15 +361,62 @@
 
         loop(b_from, col_blocks, column)
 
+    def prepare(b):
+        work[size:, :] = jnp.zeros((BASE, size), F32)
+        r_id = lax.broadcasted_iota(jnp.int32, (size + BASE, size), 0)
+        c_id = lax.broadcasted_iota(jnp.int32, (size + BASE, size), 1)
+        winv[...] = jnp.where(r_id == c_id, 1.0, 0.0).astype(F32)
+
+    def times_winv_t(x):
+        hi, mid, lo = split3(x)
+        whi, wmid, wlo = winv3[0], winv3[1], winv3[2]
+        small = times_t(lo, whi) + times_t(mid, wmid) + times_t(hi, wlo)
+        return small + (times_t(mid, whi) + times_t(hi, wmid)) + times_t(hi, whi)
+
+    def solve(k, a, count):
+        kb = k // n_col
+        here = pl.ds(spot(a, kb), count)
+
+        @pl.when(k > 0)
+        def _():
+            last = k - 1
+            for m in range(count):
+                receive(last, a + m)
+            left = panel[pl.ds(row_slot(last, a), count)].reshape(count * size, size)
+            share[here] -= times_t(left, panel[col_of(last, kb)]).reshape(count, size, size)
+
+        x = times_winv_t(share[here].reshape(count * size, size)).reshape(count, size, size)
+        panel[pl.ds(row_slot(k, a), count)] = x.astype(BF16)
+        share[here] = x
+        for m in range(count):
+            source_sends(k, a + m, start)
+        for m in range(count):
+            pltpu.make_async_copy(share.at[spot(a + m, kb)], home(o_ref, a + m, kb), store_sem).start()
+
+    @pl.when(col == 0)
+    def _():
+        prepare(0)
+        work[0:size, :] = diag[0]
+
     def step(k):
         mine = col == lax.rem(k, n_col)
         kb = k // n_col
         last = k - 1
         soon = jnp.logical_and(col == lax.rem(k + 1, n_col), k + 1 < steps)
 
-        @pl.when(jnp.logical_and(k > depth, lead(last - depth + n_col) != 0))
-        def _():
-            loop(first_passed(last - depth), row_blocks, lambda a: pass_on(last - depth, a, finish))
+        @pl.when(mine)
+        def _():
+            factor_block(work, winv, prev)
+            for n, part in enumerate(split3(winv[0:size, :])):
+                winv3[n] = part
+            lo = first_a(k)
+            single = jnp.minimum(lo + 1 + lax.rem(row_blocks - lo + 1, 2), row_blocks)
+            loop(lo, single, lambda a: solve(k, a, 1))
+            loop(0, (row_blocks - single) // 2, lambda m: solve(k, single + 2 * m, 2))
+
+        @pl.when(k >= depth)
+        def _():
+            passed(k - depth)
 
         @pl.when(k == 1)
         def _():
@@ -362,36 +425,6 @@
 
         @pl.when(mine)
         def _():
-            work[0:size, :] = diag[kb]
-            work[size:, :] = jnp.zeros((BASE, size), F32)
-            r_id = lax.broadcasted_iota(jnp.int32, (size + BASE, size), 0)
-            c_id = lax.broadcasted_iota(jnp.int32, (size + BASE, size), 1)
-            winv[...] = jnp.where(r_id == c_id, 1.0, 0.0).astype(F32)
-            factor_block(work, winv, prev)
-
-            def solve(a):
-                n = spot(a, kb)
-
-                @pl.when(k > 1)
-                def _():
-                    update_block(k - 2, a, kb)
-
-                @pl.when(k > 0)
-                def _():
-                    receive(last, a)
-                    update_block(last, a, kb)
-
-                x = lax.dot_general(
-                    share[n], winv[0:size, :], (((1,), (1,)), ((), ())), precision=lax.Precision.HIGHEST,
-                    preferred_element_type=F32,
-                )
-                panel[row_slot(k, a)] = x.astype(BF16)
-                share[n] = x
-                source_sends(k, a, start)
-                pltpu.make_async_copy(share.at[n], home(o_ref, a, kb), store_sem).start()
-
-            loop(first_a(k), row_blocks, solve)
-
             @pl.when(row == lax.rem(k, n_row))
             def _():
                 for d in range(1, n_row):
@@ -410,15 +443,13 @@
             def _():
                 trail(last, kb + 1)
 
-        @pl.when(jnp.logical_and(k > 0, jnp.logical_not(mine)))
+        @pl.when(jnp.logical_and(k > 0, jnp.logical_not(jnp.logical_or(mine, soon))))
         def _():
             @pl.when(col != lax.rem(last, n_col))
             def _():
                 loop(first_passed(last), row_blocks, lambda a: receive(last, a))
 
-            @pl.when(jnp.logical_not(soon))
-            def _():
-                trail(last, first_b(last))
+            trail(last, first_b(last))
 
         @pl.when(soon)
         def _():
@@ -426,11 +457,29 @@
 
             @pl.when(k > 0)
             def _():
+                @pl.when(on_diag)
+                def _():
+                    receive(last, (k + 1) // n_row)
+
                 column_arrived(last, nb)
                 update_diag(last, nb)
 
-            arrived(col_of(k, nb))
-            update_diag(k, nb)
+                def catch_up(a):
+                    receive(last, a)
+                    update_block(last, a, nb)
+
+                loop(first_a(k + 1), row_blocks, catch_up)
+
+            prepare(nb)
+            slot = col_of(k, nb)
+            arrived(slot)
+
+            @pl.when(on_diag)
+            def _():
+                pass_on(k, (k + 1) // n_row, start)
+
+            other = panel[slot]
+            work[0:size, :] = diag[nb] - times_t(other, other)
 
         @pl.when(jnp.logical_and(k >= n_col // 2, col == lax.rem(k + n_col // 2, n_col)))
         def _():
@@ -438,12 +487,7 @@
 
     loop(0, steps, step)
 
-    def last_passes(p):
-        @pl.when(lead(p) != 0)
-        def _():
-            loop(first_passed(p), row_blocks, lambda a: pass_on(p, a, finish))
-
-    loop(steps - 1 - depth, steps - 1, last_passes)
+    loop(steps - depth, steps, passed)
 
     def last_sends(k):
         @pl.when(col == lax.rem(k, n_col))
@@ -473,6 +517,7 @@
                 pltpu.VMEM((slots, size, size), BF16),
                 pltpu.VMEM((size + BASE, size), F32),
                 pltpu.VMEM((size + BASE, size), F32),
+                pltpu.VMEM((3, size, size), BF16),
                 pltpu.VMEM((BASE, 3 * LANE), F32),
                 pltpu.SemaphoreType.DMA,
                 pltpu.SemaphoreType.DMA,

time: 439 us -> 449 us (1.023)
  Pallas kernels: 430 us -> 440 us
    pallas_call x1, Pallas kernels: 430 us -> 440 us  [factor_local(): pl.pallas_call(functools.partial(kernel, n_row, n_col, 'batch'), out_shap...]
where the time goes in v3:
time: 449 us; the launch traced here: 448 us
  Pallas kernels  440 us (98%)
  local copies, waits for them, and re-layouts  8.44 us (2%)
    pallas_call x1, Pallas kernels, factor_local(): pl.pallas_call(functools.partial(kernel, n_row, n_col, 'batch'), out_shap...  440 us

profile of v3, /device:TPU:103, one launch (start us, length us, event | category | flops | bytes accessed | tf_op | source)
XLA Modules:
  0.0 448.3 jit_solution(14604344739964970925)
XLA Ops:
  0.0 439.9 %cholesky.1 = f32[8,256,1024]{2,1,0:T(8,128)} custom-call(f32[8,256,1024]{2,1,0:T(8,128)} %a_ref.1), custom_call_target="tpu_custom_call" | custom-call | tf_op jit(solution)/shard_map/cholesky/pallas_call | solution.py:509
  439.9 8.4 %copy.3 = f32[8,256,1024]{2,1,0:T(8,128)} copy(f32[8,256,1024]{2,1,0:T(8,128)} %cholesky.1) | data formatting | bytes 16777216
